TPU v7x, 32 devices: a whole 2x2x4 slice. The times are simulated.
32 devices in a mesh: group: 8 (over z, x), peer: 4 (over y, core).
Axes of the slice: x: 2, y: 2, z: 4, core: 2. Of those that a mesh axis runs over, the one named last changes fastest.
Arguments:
- features: bfloat16 [12288, 1024], P(('group', 'peer')), may hold values from -6 to 6
- task_mask: int32 [12288], P(('group', 'peer')), may hold values from 0 to 65535, as said below
- tower_in: bfloat16 [16, 2048, 1024], P('peer', 'group'), may hold values from -0.1875 to 0.1875
- tower_bias: bfloat16 [16, 2048], P('peer', 'group'), may hold values from -5 to 5
- tower_head: bfloat16 [16, 2048], P('peer', 'group'), may hold values from -0.125 to 0.125
- head_bias: float32 [16], P('peer'), may hold values from -4 to 4
Outputs:
- predictions: float32 [12288, 16], P(('group', 'peer'))
Inputs may be any that keep to these rules, and one draw needn't show every extreme that they name: `task_mask`: only bits 0 to 15 are used. Among the 384 samples of one device (aligned blocks of 384), at most 176 have any one bit set; in every run of 4 blocks that one group holds, some task's bit is set exactly 176 times in each block.
All inputs are finite; a program needn't handle non-finite values.
Results may differ from a plain program's by a relative error of at most 0.0003.
Values may be sent and summed in bfloat16 or wider, within the bound.
A program may use at most 128 MiB of HBM per device.

v0:
```python
import jax
import jax.numpy as jnp
from jax import lax
from jax.sharding import PartitionSpec as P

CAP = 176


def shards(features, task_mask, tower_in, tower_bias, tower_head, head_bias):
    peers = lax.axis_size("peer")
    local_tasks = tower_in.shape[0]
    all_tasks = local_tasks * peers
    task_ids = jnp.arange(all_tasks, dtype=jnp.int32)
    slot_indices = jnp.arange(CAP, dtype=jnp.int32)
    task_bits = task_mask[:, None] >> task_ids[None, :] & 1
    inclusive = jnp.cumsum(task_bits, axis=0)
    slot_rank = inclusive - task_bits
    task_selector = (slot_rank.T[:, None, :] == slot_indices[None, :, None]) & (
        task_bits.T[:, None, :] == 1
    )
    outgoing = jnp.einsum(
        "yra,az->yrz",
        task_selector.astype(jnp.bfloat16),
        features,
        preferred_element_type=jnp.float32,
    ).astype(jnp.bfloat16)
    outgoing = outgoing.reshape(peers, local_tasks, CAP, features.shape[1])
    arrived = lax.all_to_all(outgoing, "peer", split_axis=0, concat_axis=0, tiled=True)
    weight = lax.all_gather(tower_in, "group", axis=1, tiled=True)
    hidden_unit_bias = lax.all_gather(tower_bias, "group", axis=1, tiled=True)
    head_row = lax.all_gather(tower_head, "group", axis=1, tiled=True)
    preact = jnp.einsum("sjcd,jhd->sjch", arrived, weight, preferred_element_type=jnp.float32)
    hidden = jnp.maximum(preact + hidden_unit_bias.astype(jnp.float32)[None, :, None, :], 0.0)
    logits = jnp.einsum(
        "sjch,jh->sjc", hidden, head_row.astype(jnp.float32), precision=lax.Precision.HIGHEST
    )
    logits = logits + head_bias[None, :, None]
    returned_output = lax.all_to_all(
        logits, "peer", split_axis=0, concat_axis=0, tiled=True
    ).reshape(all_tasks, CAP)
    task_selector = (slot_rank.T[:, None, :] == slot_indices[None, :, None]) & (
        task_bits.T[:, None, :] == 1
    )
    return jnp.einsum(
        "ivf,iv->fi",
        task_selector.astype(jnp.float32),
        returned_output,
        precision=lax.Precision.HIGHEST,
    )


def solution(mesh):
    placed = (
        P(("group", "peer"), None),
        P(("group", "peer")),
        P("peer", "group", None),
        P("peer", "group"),
        P("peer", "group"),
        P("peer"),
    )
    return jax.shard_map(
        shards, mesh=mesh, in_specs=placed, out_specs=P(("group", "peer"), None), check_vma=False
    )
```

profile of v0, /device:TPU:0, one launch (start us, length us, event | category | flops | bytes accessed | tf_op | source)
XLA Modules:
  0.0 291.0 jit_solution(16052179998820379908)
XLA Ops:
  6.5 0.0 copy-start
  6.5 0.0 all-gather.2.cloned.1.call-start
  6.5 0.7 all-gather.2.cloned.1.call-update
  7.3 0.7 shift-right-arithmetic_and_fusion.1
  7.9 0.9 reduce-window.6
  8.8 0.2 slice_reduce_fusion
  9.1 0.7 fusion.23
  9.8 0.8 bitcast_subtract_fusion
  10.5 0.0 copy-done
  10.5 4.9 %fusion.14 = bf16[16,176,1024]{2,1,0:T(8,128)(2,1)} fusion(s32[16,384]{1,0:T(8,128)S(1)} %bitcast_subtract_fusion, pred[16,384]{1,0:T(8,128)(4,1)S(1)} %fusion.23, bf16[384,1024]{1,0:T(8,128)(2,1)S(1)} %copy-done), kind=kOutput, calls=%fused_computation.13 | convolution fusion | flops 2219638784 | bytes 6584320 | tf_op jit(solution)/shard_map/yra,az->yrz/dot_general | solution.py:21
  15.4 0.0 copy-start.1
  15.4 0.0 copy-start.2
  15.4 5.3 %all-to-all-start = ((bf16[4,4,176,1024]{3,2,1,0:T(8,128)(2,1)}), bf16[4,4,176,1024]{3,2,1,0:T(8,128)(2,1)}, u32[]{:S(2)}, u32[]{:S(2)}) async-start(bf16[4,4,176,1024]{3,2,1,0:T(8,128)(2,1)} %bitcast.32), calls=%async_computation | async-start | bytes 11534336 | tf_op jit(solution)/shard_map/all_to_all | solution.py:28
  20.7 0.0 copy-done.1
  20.7 29.4 %all_gather.10 = bf16[4,2048]{1,0:T(4,128)(2,1)S(1)} all-gather(bf16[4,256]{1,0:T(4,128)(2,1)S(1)} %copy-done.1), channel_id=1, replica_groups=mesh['group'=8,'peer'=4] {'group'}, dimensions={1}, use_global_device_ids=true | all-gather | bytes 18432 | tf_op jit(solution)/shard_map/all_gather | solution.py:30
  50.2 0.0 copy-done.2
  50.2 27.3 %all_gather.11 = bf16[4,2048]{1,0:T(4,128)(2,1)S(1)} all-gather(bf16[4,256]{1,0:T(4,128)(2,1)S(1)} %copy-done.2), channel_id=1, replica_groups=mesh['group'=8,'peer'=4] {'group'}, dimensions={1}, use_global_device_ids=true | all-gather | bytes 18432 | tf_op jit(solution)/shard_map/all_gather | solution.py:31
  77.5 9.2 %all-to-all-done = bf16[4,4,176,1024]{3,2,1,0:T(8,128)(2,1)} async-done(((bf16[4,4,176,1024]{3,2,1,0:T(8,128)(2,1)}), bf16[4,4,176,1024]{3,2,1,0:T(8,128)(2,1)}, u32[]{:S(2)}, u32[]{:S(2)}) %all-to-all-start) | async-done | bytes 5767200 | tf_op jit(solution)/shard_map/all_to_all | solution.py:28
  86.7 153.3 %all-gather.2.cloned.1.call-done = bf16[4,2048,1024]{2,1,0:T(8,128)(2,1)} async-done(((bf16[4,256,1024]{2,1,0:T(8,128)(2,1)}), bf16[4,2048,1024]{2,1,0:T(8,128)(2,1)}) %all-gather.2.cloned.1.call-update) | async-done | bytes 16777232 | tf_op jit(solution)/shard_map/all_gather | solution.py:29
  240.0 20.6 %fusion.4 = f32[4,4,176,2048]{3,2,1,0:T(8,128)} fusion(bf16[4,2048,1024]{2,1,0:T(8,128)(2,1)} %all-gather.2.cloned.1.call-done, bf16[4,4,176,1024]{3,2,1,0:T(8,128)(2,1)} %all-to-all-done), kind=kOutput, calls=%fused_computation.4 | convolution fusion | flops 11811160064 | bytes 45613056 | tf_op jit(solution)/shard_map/sjcd,jhd->sjch/dot_general | solution.py:32
  260.6 0.0 copy-start.3
  260.6 14.7 %fusion = f32[4,1,4,176]{3,1,2,0:T(1,128)S(1)} fusion(f32[4,4,176,2048]{3,2,1,0:T(8,128)} %fusion.4, f32[4,2048]{1,0:T(4,128)S(1)} %convert_element_type.10, bf16[4,2048,1,1]{1,0,2,3:T(4,128)(2,1)S(1)} %bitcast.33), kind=kOutput, calls=%fused_computation | convolution fusion | flops 80740352 | bytes 23129088 | tf_op jit(solution)/shard_map/sjch,jh->sjc/dot_general | solution.py:34
  275.3 0.0 copy-done.3
  275.3 0.1 fusion.24
  275.4 6.4 %all_to_all.10 = f32[4,4,176]{2,1,0:T(4,128)S(1)} all-to-all(f32[4,4,176]{2,1,0:T(4,128)S(1)} %fusion.24), channel_id=1, replica_groups=mesh['group'=8,'peer'=4] {'peer'}, dimensions={0} | all-to-all | bytes 22528 | tf_op jit(solution)/shard_map/all_to_all | solution.py:38
  281.8 1.8 fusion.10
  283.6 0.6 copy.22
  (3 shorter events, 0.1 us)
Async XLA Ops:
  6.5 4.0 %copy-start = (bf16[384,1024]{1,0:T(8,128)(2,1)S(1)}, bf16[384,1024]{1,0:T(8,128)(2,1)}, u32[]{:S(2)}) copy-start(bf16[384,1024]{1,0:T(8,128)(2,1)} %param.6) | copy-start | bytes 2359300
  6.5 233.5 %all-gather.2.cloned.1.call-start = ((), (), s32[]{:S(2)}) async-start(), calls=%async_computation.2 | async-start | bytes 18874368 | tf_op jit(solution)/shard_map/all_gather | solution.py:29
  15.4 5.3 %copy-start.1 = (bf16[4,256]{1,0:T(4,128)(2,1)S(1)}, bf16[4,256]{1,0:T(4,128)(2,1)}, u32[]{:S(2)}) copy-start(bf16[4,256]{1,0:T(4,128)(2,1)} %param.9) | copy-start | bytes 6148
  15.4 34.7 %copy-start.2 = (bf16[4,256]{1,0:T(4,128)(2,1)S(1)}, bf16[4,256]{1,0:T(4,128)(2,1)}, u32[]{:S(2)}) copy-start(bf16[4,256]{1,0:T(4,128)(2,1)} %param.10) | copy-start | bytes 6148
  15.4 71.2 %all-to-all-start = ((bf16[4,4,176,1024]{3,2,1,0:T(8,128)(2,1)}), bf16[4,4,176,1024]{3,2,1,0:T(8,128)(2,1)}, u32[]{:S(2)}, u32[]{:S(2)}) async-start(bf16[4,4,176,1024]{3,2,1,0:T(8,128)(2,1)} %bitcast.32), calls=%async_computation | async-start | bytes 11534336 | tf_op jit(solution)/shard_map/all_to_all | solution.py:28
  260.6 14.7 %copy-start.3 = (f32[4]{0:T(128)S(1)}, f32[4]{0:T(128)}, u32[]{:S(2)}) copy-start(f32[4]{0:T(128)} %param.11) | copy-start | bytes 52
Sparse Core Ops, SparseCore 0:
  9.5 230.4 all-gather.1
where the time goes:
time: 291 us
  waiting for transfers between devices  163 us (56%)
  blocking collectives  63.1 us (22%)
  matrix products  42 us (14%)
  between operations  13.4 us (5%)
  starting transfers between devices  5.26 us (2%)
  other arithmetic  3.12 us (1%)
    all_gather x1, waiting for transfers between devices, shards(): weight = lax.all_gather(tower_in, 'group', axis=1, tiled=True)  153 us
    all_gather x1, blocking collectives, shards(): hidden_unit_bias = lax.all_gather(tower_bias, 'group', axis=1, tiled=True)  29.4 us
    all_gather x1, blocking collectives, shards(): head_row = lax.all_gather(tower_head, 'group', axis=1, tiled=True)  27.3 us
    dot_general x1, matrix products, shards(): jnp.einsum('sjcd,jhd->sjch', arrived, weight, preferred_element_type=jnp....  20.6 us
    dot_general x1, matrix products, shards(): jnp.einsum('sjch,jh->sjc', hidden, head_row.astype(jnp.float32), precisio...  14.7 us
    all_to_all x1, waiting for transfers between devices, shards(): lax.all_to_all(outgoing, 'peer', split_axis=0, concat_axis=0, tiled=True)  9.23 us
    all_to_all x1, blocking collectives, shards(): lax.all_to_all(logits, 'peer', split_axis=0, concat_axis=0, tiled=True)  6.38 us
  transfers between devices with their start and end apart: 2, of which 2 were waited for; matrix products, arithmetic and copies ran while one was open for 3% of the time, Pallas kernels for 0%

commit v1 on v0

--- a/solution.py
+++ b/solution.py
@@ -4,6 +4,12 @@
 from jax.sharding import PartitionSpec as P
 
 CAP = 176
+
+
+def all_parts(block, name, along):
+    parts = lax.all_gather(block, name, axis=0, tiled=False)
+    result = jnp.concatenate(parts, axis=along)
+    return result
 
 
 def shards(features, task_mask, tower_in, tower_bias, tower_head, head_bias):
@@ -26,7 +32,7 @@
     ).astype(jnp.bfloat16)
     outgoing = outgoing.reshape(peers, local_tasks, CAP, features.shape[1])
     arrived = lax.all_to_all(outgoing, "peer", split_axis=0, concat_axis=0, tiled=True)
-    weight = lax.all_gather(tower_in, "group", axis=1, tiled=True)
+    weight = all_parts(tower_in, "group", 1)
     hidden_unit_bias = lax.all_gather(tower_bias, "group", axis=1, tiled=True)
     head_row = lax.all_gather(tower_head, "group", axis=1, tiled=True)
     preact = jnp.einsum("sjcd,jhd->sjch", arrived, weight, preferred_element_type=jnp.float32)

time: 291 us -> 305 us (1.048)
  local copies, waits for them, and re-layouts: 0.88 us -> 14.7 us
    reshape x0 -> x1, local copies, waits for them, and re-layouts: none -> 13.9 us  [all_parts(): result = jnp.concatenate(parts, axis=along)]
    all_to_all x1, waiting for transfers between devices: 9.23 us -> 0.01 us  [shards(): lax.all_to_all(outgoing, 'peer', split_axis=0, concat_axis=0, tiled=True)]
    all_gather x1, waiting for transfers between devices: 153 us -> 161 us  [all_parts(): parts = lax.all_gather(block, name, axis=0, tiled=False)]
  transfers between devices with their start and end apart: 2 -> 2, of which waited for: 2 -> 1; matrix products, arithmetic and copies ran while one was open for 3% -> 7% of each run, Pallas kernels for 0% -> 0%
where the time goes in v1:
time: 305 us
  waiting for transfers between devices  162 us (53%)
  blocking collectives  64.9 us (21%)
  matrix products  42 us (14%)
  local copies, waits for them, and re-layouts  14.7 us (5%)
  between operations  13.4 us (4%)
  starting transfers between devices  5.28 us (2%)
  other arithmetic  3.12 us (1%)
    all_gather x1, waiting for transfers between devices, all_parts(): parts = lax.all_gather(block, name, axis=0, tiled=False)  161 us
    all_gather x1, blocking collectives, shards(): hidden_unit_bias = lax.all_gather(tower_bias, 'group', axis=1, tiled=True)  31.2 us
    all_gather x1, blocking collectives, shards(): head_row = lax.all_gather(tower_head, 'group', axis=1, tiled=True)  27.3 us
    dot_general x1, matrix products, shards(): jnp.einsum('sjcd,jhd->sjch', arrived, weight, preferred_element_type=jnp....  20.6 us
    dot_general x1, matrix products, shards(): jnp.einsum('sjch,jh->sjc', hidden, head_row.astype(jnp.float32), precisio...  14.8 us
    reshape x1, local copies, waits for them, and re-layouts, all_parts(): result = jnp.concatenate(parts, axis=along)  13.9 us
    all_to_all x1, blocking collectives, shards(): lax.all_to_all(logits, 'peer', split_axis=0, concat_axis=0, tiled=True)  6.39 us
  transfers between devices with their start and end apart: 2, of which 1 were waited for; matrix products, arithmetic and copies ran while one was open for 7% of the time, Pallas kernels for 0%

profile of v1, /device:TPU:0, one launch (start us, length us, event | category | flops | bytes accessed | tf_op | source)
XLA Modules:
  0.0 305.0 jit_solution(15945945430129793686)
XLA Ops:
  6.5 0.0 copy-start
  6.5 0.0 all-gather.3.cloned.1.call-start
  6.5 0.7 all-gather.3.cloned.1.call-update
  7.3 0.7 shift-right-arithmetic_and_fusion.1
  7.9 0.9 reduce-window.6
  8.8 0.2 slice_reduce_fusion
  9.1 0.7 fusion.22
  9.8 0.8 bitcast_subtract_fusion
  10.5 0.0 copy-done
  10.5 4.9 %fusion.13 = bf16[16,176,1024]{2,1,0:T(8,128)(2,1)} fusion(s32[16,384]{1,0:T(8,128)S(1)} %bitcast_subtract_fusion, pred[16,384]{1,0:T(8,128)(4,1)S(1)} %fusion.22, bf16[384,1024]{1,0:T(8,128)(2,1)S(1)} %copy-done), kind=kOutput, calls=%fused_computation.12 | convolution fusion | flops 2219638784 | bytes 6584320 | tf_op jit(solution)/shard_map/yra,az->yrz/dot_general | solution.py:27
  15.4 0.0 copy-start.2
  15.4 0.0 copy-start.3
  15.4 5.3 %all-to-all-start = ((bf16[4,4,176,1024]{3,2,1,0:T(8,128)(2,1)}), bf16[4,4,176,1024]{3,2,1,0:T(8,128)(2,1)}, u32[]{:S(2)}, u32[]{:S(2)}) async-start(bf16[4,4,176,1024]{3,2,1,0:T(8,128)(2,1)} %bitcast.38), calls=%async_computation | async-start | bytes 11534336 | tf_op jit(solution)/shard_map/all_to_all | solution.py:34
  20.7 0.0 copy-done.2
  20.7 31.2 %all_gather.14 = bf16[4,2048]{1,0:T(4,128)(2,1)S(1)} all-gather(bf16[4,256]{1,0:T(4,128)(2,1)S(1)} %copy-done.2), channel_id=1, replica_groups=mesh['group'=8,'peer'=4] {'group'}, dimensions={1}, use_global_device_ids=true | all-gather | bytes 18432 | tf_op jit(solution)/shard_map/all_gather | solution.py:36
  51.9 0.0 copy-done.3
  51.9 27.3 %all_gather.15 = bf16[4,2048]{1,0:T(4,128)(2,1)S(1)} all-gather(bf16[4,256]{1,0:T(4,128)(2,1)S(1)} %copy-done.3), channel_id=1, replica_groups=mesh['group'=8,'peer'=4] {'group'}, dimensions={1}, use_global_device_ids=true | all-gather | bytes 18432 | tf_op jit(solution)/shard_map/all_gather | solution.py:37
  79.2 160.8 %all-gather.3.cloned.1.call-done = bf16[32,256,1024]{2,1,0:T(8,128)(2,1)} async-done(((bf16[4,256,1024]{2,1,0:T(8,128)(2,1)}), bf16[32,256,1024]{2,1,0:T(8,128)(2,1)}) %all-gather.3.cloned.1.call-update) | async-done | bytes 16777232 | tf_op jit(solution)/shard_map/all_gather | solution.py:10
  240.0 13.9 %copy.12 = bf16[4,8,256,1024]{3,2,1,0:T(8,128)(2,1)} copy(bf16[4,8,256,1024]{3,2,0,1:T(8,128)(2,1)} %bitcast.36) | data formatting | bytes 33554432 | tf_op jit(solution)/shard_map/reshape | solution.py:11
  253.9 0.0 all-to-all-done
  253.9 20.6 %fusion.6 = f32[4,4,176,2048]{3,2,1,0:T(8,128)} fusion(bf16[4,2048,1024,1]{2,1,3,0:T(8,128)(2,1)} %bitcast.37, bf16[4,4,176,1024]{3,2,1,0:T(8,128)(2,1)} %all-to-all-done), kind=kOutput, calls=%fused_computation.6 | convolution fusion | flops 11811160064 | bytes 45613056 | tf_op jit(solution)/shard_map/sjcd,jhd->sjch/dot_general | solution.py:38
  274.5 0.0 copy-start.4
  274.5 0.0 copy-start.1
  274.5 14.8 %fusion = f32[4,1,4,176]{3,1,2,0:T(1,128)S(1)} fusion(f32[4,4,176,2048]{3,2,1,0:T(8,128)} %fusion.6, f32[4,2048]{1,0:T(4,128)S(1)} %convert_element_type.10, bf16[4,2048,1,1]{1,0,2,3:T(4,128)(2,1)S(1)} %bitcast.39), kind=kOutput, calls=%fused_computation | convolution fusion | flops 80740352 | bytes 23129088 | tf_op jit(solution)/shard_map/sjch,jh->sjc/dot_general | solution.py:40
  289.3 0.0 copy-done.4
  289.3 0.1 fusion.23
  289.3 6.4 %all_to_all.10 = f32[4,4,176]{2,1,0:T(4,128)S(1)} all-to-all(f32[4,4,176]{2,1,0:T(4,128)S(1)} %fusion.23), channel_id=1, replica_groups=mesh['group'=8,'peer'=4] {'peer'}, dimensions={0} | all-to-all | bytes 22528 | tf_op jit(solution)/shard_map/all_to_all | solution.py:44
  295.8 1.8 fusion.9
  297.6 0.6 copy.27
  298.2 0.0 copy-done.1
  (3 shorter events, 0.1 us)
Async XLA Ops:
  6.5 4.0 %copy-start = (bf16[384,1024]{1,0:T(8,128)(2,1)S(1)}, bf16[384,1024]{1,0:T(8,128)(2,1)}, u32[]{:S(2)}) copy-start(bf16[384,1024]{1,0:T(8,128)(2,1)} %param.6) | copy-start | bytes 2359300
  6.5 233.5 %all-gather.3.cloned.1.call-start = ((), (), s32[]{:S(2)}) async-start(), calls=%async_computation.2 | async-start | bytes 18874368 | tf_op jit(solution)/shard_map/all_gather | solution.py:10
  15.4 5.3 %copy-start.2 = (bf16[4,256]{1,0:T(4,128)(2,1)S(1)}, bf16[4,256]{1,0:T(4,128)(2,1)}, u32[]{:S(2)}) copy-start(bf16[4,256]{1,0:T(4,128)(2,1)} %param.9) | copy-start | bytes 6148
  15.4 36.5 %copy-start.3 = (bf16[4,256]{1,0:T(4,128)(2,1)S(1)}, bf16[4,256]{1,0:T(4,128)(2,1)}, u32[]{:S(2)}) copy-start(bf16[4,256]{1,0:T(4,128)(2,1)} %param.10) | copy-start | bytes 6148
  15.4 238.5 %all-to-all-start = ((bf16[4,4,176,1024]{3,2,1,0:T(8,128)(2,1)}), bf16[4,4,176,1024]{3,2,1,0:T(8,128)(2,1)}, u32[]{:S(2)}, u32[]{:S(2)}) async-start(bf16[4,4,176,1024]{3,2,1,0:T(8,128)(2,1)} %bitcast.38), calls=%async_computation | async-start | bytes 11534336 | tf_op jit(solution)/shard_map/all_to_all | solution.py:34
  274.5 14.8 %copy-start.4 = (f32[4]{0:T(128)S(1)}, f32[4]{0:T(128)}, u32[]{:S(2)}) copy-start(f32[4]{0:T(128)} %param.11) | copy-start | bytes 52
  274.5 23.7 %copy-start.1 = (bf16[384,1024]{1,0:T(8,128)(2,1)S(1)}, bf16[384,1024]{1,0:T(8,128)(2,1)}, u32[]{:S(2)}) copy-start(bf16[384,1024]{1,0:T(8,128)(2,1)} %param.6) | copy-start | bytes 2359300
Sparse Core Ops, SparseCore 0:
  9.5 230.5 all-gather.2
